TPU v7x, 32 devices: a whole 2x2x4 slice. The times are simulated.
32 devices in a mesh: gene: 4 (over y, x), prot: 8 (over z, core).
Axes of the slice: x: 2, y: 2, z: 4, core: 2. Of those that a mesh axis runs over, the one named last changes fastest.
Arguments:
- density: float32 [256, 48, 16, 128], P('gene', 'prot'), may hold values from 0 to 2
- levels: float32 [8], replicated, may hold values from 0.1 to 0.9
- rate_index: int32 [256, 3], P('gene'), may hold values from 0 to 7
- on_rate: float32 [8], replicated, may hold values from 0.2 to 3
- off_rate: float32 [8], replicated, may hold values from 0.2 to 3
- gene_order: int32 [4], replicated, may hold values from 0 to 3, each once
Outputs:
- evolved: float32 [256, 48, 16, 128], P('gene', 'prot')
Inputs may be any that keep to these rules, and one draw needn't show every extreme that they name: `gene_order`: a permutation of 0 to 3.
All inputs are finite; a program needn't handle non-finite values.
Results may differ from a plain program's by a relative error of at most 0.00002.
Values sent between devices are 32-bit elements; how exact they have to be, the bound alone decides.
A program may use at most 128 MiB of HBM per device.

v0:
```python
from functools import partial

import jax
import jax.numpy as jnp
from jax import lax
from jax.sharding import PartitionSpec as P

STATE_BITS = 8
BLOCKS = 4
SUBSTEPS = 6


DIFF = 1.0
TIME_STEP = 0.15


def partner(value, axis, apart):
    mask = 2**apart
    pairs = [(source, source ^ mask) for source in range(lax.axis_size(axis))]
    return lax.ppermute(value, axis, pairs)


def extended(cells, sides, width):
    for axis, dim in sides:
        count = lax.axis_size(axis)
        ends = count - 1
        head = lax.slice_in_dim(cells, 0, width, axis=dim)
        tail = lax.slice_in_dim(cells, cells.shape[dim] - width, cells.shape[dim], axis=dim)
        cells = jnp.concatenate(
            [
                lax.ppermute(tail, axis, [(i, (i + 1) % count) for i in range(ends)]),
                cells,
                lax.ppermute(head, axis, [((i + 1) % count, i) for i in range(ends)]),
            ],
            axis=dim,
        )
    return cells


def along(field, drift, axis):
    pads = [(0, 0)] * 4
    pads[axis] = (1, 1)
    padded = jnp.pad(field, pads)
    dpad = jnp.pad(drift, pads)
    size = field.shape[axis]
    upper = lax.slice_in_dim(padded, 2, size + 2, axis=axis)
    lower = lax.slice_in_dim(padded, 0, size, axis=axis)
    d_up = lax.slice_in_dim(dpad, 2, size + 2, axis=axis)
    d_low = lax.slice_in_dim(dpad, 0, size, axis=axis)
    return DIFF * (upper - 2.0 * field + lower) - 0.5 * (d_up * upper - d_low * lower)


def substep(field, drift_x, drift_y, drift_z):
    change = along(field, drift_x, 1) + along(field, drift_y, 2) + along(field, drift_z, 3)
    return field + TIME_STEP * change


def partner_of(field, bit, local_bits):
    if bit < local_bits:
        count = field.shape[0]
        grouped = field.reshape((count >> bit + 1, 2, 1 << bit) + field.shape[1:])
        return grouped[:, ::-1].reshape(field.shape)
    return partner(field, "gene", bit - local_bits)


def local(density, levels, rate_index, on_rate, off_rate, gene_order):
    count, width_x, size_y, size_z = density.shape
    local_bits = count.bit_length() - 1
    total_x = width_x * lax.axis_size("prot")
    first_x = lax.axis_index("prot") * width_x
    state_ids = lax.axis_index("gene") * count + jnp.arange(count, dtype=jnp.int32)
    onehot = rate_index[:, :, None] == jnp.arange(levels.shape[0], dtype=jnp.int32)[None, None, :]
    level_of = jnp.sum(jnp.where(onehot, levels[None, None, :], 0.0), axis=-1)
    coord_y = (jnp.arange(size_y, dtype=jnp.float32) + 0.5) / size_y
    coord_z = (jnp.arange(size_z, dtype=jnp.float32) + 0.5) / size_z
    drift_y = (level_of[:, 1, None] - coord_y[None, :])[:, None, :, None]
    drift_z = (level_of[:, 2, None] - coord_z[None, :])[:, None, None, :]
    own_x = (first_x + jnp.arange(width_x, dtype=jnp.int32)).astype(jnp.float32)
    own_x = (own_x + 0.5) / total_x
    hill = 0.1 + own_x**2 / (0.09 + own_x**2)
    branches = [
        partial(partner_of, bit=STATE_BITS - 1 - k, local_bits=local_bits) for k in range(BLOCKS)
    ]
    field = density
    for block in range(BLOCKS):
        cells = first_x - SUBSTEPS + jnp.arange(width_x + 2 * SUBSTEPS, dtype=jnp.int32)
        inside = ((cells >= 0) & (cells < total_x)).astype(jnp.float32)[None, :, None, None]
        coord = (cells.astype(jnp.float32) + 0.5) / total_x
        drift_x, inside = ((level_of[:, 0, None] - coord[None, :])[:, :, None, None], inside)
        wide = extended(field, (("prot", 1),), SUBSTEPS)
        for step in range(SUBSTEPS):
            wide = substep(wide, drift_x, drift_y, drift_z) * inside
        field = wide[:, SUBSTEPS : SUBSTEPS + width_x]
        bit = STATE_BITS - 1 - gene_order[block]
        mate = lax.switch(gene_order[block], branches, field)
        high = (jnp.bitwise_and(jnp.right_shift(state_ids, bit), 1) == 1)[:, None, None, None]
        act = (on_rate[bit] * hill)[None, :, None, None]
        rate = act + off_rate[bit]
        share = act / rate
        decay = jnp.exp(-rate)
        low_part = jnp.where(high, mate, field)
        high_part = jnp.where(high, field, mate)
        total = low_part + high_part
        new_high = share * total + (high_part - share * total) * decay
        field = jnp.where(high, new_high, total - new_high)
    return field


def solution(mesh):
    in_specs = (P("gene", "prot", None, None), P(), P("gene", None), P(), P(), P())
    out_specs = P("gene", "prot", None, None)
    return jax.shard_map(local, mesh=mesh, in_specs=in_specs, out_specs=out_specs, check_vma=False)
```

profile of v0, /device:TPU:9, one launch (start us, length us, event | category | flops | bytes accessed | tf_op | source)
XLA Modules:
  0.0 1144.2 jit_solution(154689823079710855)
XLA Ops:
  0.0 3.8 collective-permute-start.8
  18.3 20.0 %collective-permute-done.8 = f32[64,6,16,128]{3,2,1,0:T(8,128)} collective-permute-done((f32[64,6,16,128]{3,2,1,0:T(8,128)}, f32[64,6,16,128]{3,2,1,0:T(8,128)}, u32[]{:S(2)}, u32[]{:S(2)}) %collective-permute-start.8) | collective-permute-done | bytes 3145760 | tf_op jit(solution)/shard_map/ppermute | solution.py:31
  42.8 3.6 copy-done
  46.4 30.5 %add_multiply_fusion.19 = f32[64,18,16,128]{3,2,1,0:T(8,128)S(1)} fusion(f32[64,18,16,128]{3,2,1,0:T(8,128)} %copy-done, f32[18]{0:T(128)S(1)} %and_convert_fusion, f32[64,128]{1,0:T(8,128)S(1)} %get-tuple-element.74, f32[64,128]{1,0:T(8,128)S(1)} %get-tuple-element.73, f32[64,16]{1,0:T(8,128)S(1)} %get-tuple-element.72, ...), kind=kLoop, calls=%fused_computation.243 | loop fusion | flops 63700992 | bytes 18957384 | tf_op jit(solution)/shard_map/mul | solution.py:92
  77.0 14.8 %add_multiply_fusion.18 = f32[64,18,16,128]{3,2,1,0:T(8,128)} fusion(f32[64,18,16,128]{3,2,1,0:T(8,128)S(1)} %add_multiply_fusion.19, f32[18]{0:T(128)S(1)} %and_convert_fusion, f32[64,128]{1,0:T(8,128)S(1)} %get-tuple-element.74, f32[64,128]{1,0:T(8,128)S(1)} %get-tuple-element.73, f32[64,16]{1,0:T(8,128)S(1)} %get-tuple-element.72, ...), kind=kLoop, calls=%fused_computation.239 | loop fusion | flops 63700992 | bytes 18957384 | tf_op jit(solution)/shard_map/mul | solution.py:92
  91.8 30.5 %add_multiply_fusion.17 = f32[64,18,16,128]{3,2,1,0:T(8,128)S(1)} fusion(f32[64,18,16,128]{3,2,1,0:T(8,128)} %add_multiply_fusion.18, f32[18]{0:T(128)S(1)} %and_convert_fusion, f32[64,128]{1,0:T(8,128)S(1)} %get-tuple-element.74, f32[64,128]{1,0:T(8,128)S(1)} %get-tuple-element.73, f32[64,16]{1,0:T(8,128)S(1)} %get-tuple-element.72, ...), kind=kLoop, calls=%fused_computation.235 | loop fusion | flops 63700992 | bytes 18957384 | tf_op jit(solution)/shard_map/mul | solution.py:92
  122.3 14.7 %add_multiply_fusion.16 = f32[64,18,16,128]{3,2,1,0:T(8,128)} fusion(f32[64,18,16,128]{3,2,1,0:T(8,128)S(1)} %add_multiply_fusion.17, f32[18]{0:T(128)S(1)} %and_convert_fusion, f32[64,128]{1,0:T(8,128)S(1)} %get-tuple-element.74, f32[64,128]{1,0:T(8,128)S(1)} %get-tuple-element.73, f32[64,16]{1,0:T(8,128)S(1)} %get-tuple-element.72, ...), kind=kLoop, calls=%fused_computation.231 | loop fusion | flops 63700992 | bytes 18957384 | tf_op jit(solution)/shard_map/mul | solution.py:92
  137.1 32.8 %add_multiply_fusion.15 = f32[64,18,16,128]{3,2,1,0:T(8,128)} fusion(f32[64,18,16,128]{3,2,1,0:T(8,128)} %add_multiply_fusion.16, f32[18]{0:T(128)S(1)} %and_convert_fusion, f32[64,128]{1,0:T(8,128)S(1)} %get-tuple-element.74, f32[64,128]{1,0:T(8,128)S(1)} %get-tuple-element.73, f32[64,16]{1,0:T(8,128)S(1)} %get-tuple-element.72, ...), kind=kLoop, calls=%fused_computation.227 | loop fusion | flops 63700992 | bytes 18957384 | tf_op jit(solution)/shard_map/mul | solution.py:92
  169.9 65.8 %subtract_add_fusion.7 = (f32[64,18,16,128]{3,2,1,0:T(8,128)}, f32[64,18,16,128]{3,2,1,0:T(8,128)}, f32[64,18,16,128]{3,2,1,0:T(8,128)}, f32[64,18,16,128]{3,2,1...) fusion(f32[64,18,16,128]{3,2,1,0:T(8,128)} %add_multiply_fusion.15, ...), kind=kLoop, calls=%fused_computation.226 | loop fusion | flops 40108032 | bytes 75580416 | tf_op jit(solution)/shard_map/add | solution.py:50
  235.7 9.3 fusion.55
  246.9 3.1 subtract_select_fusion.3
  250.0 4.3 collective-permute-start.10
  259.6 28.9 %collective-permute-done.10 = f32[64,6,16,128]{3,2,1,0:T(8,128)S(1)} collective-permute-done((f32[64,6,16,128]{3,2,1,0:T(8,128)S(1)}, f32[64,6,16,128]{3,2,1,0:T(8,128)S(1)}, u32[]{:S(2)}, u32[]{:S(2)}) %collective-permute-start.10) | collective-permute-done | bytes 3145760 | tf_op jit(solution)/shard_map/ppermute | solution.py:31
  288.5 4.5 collective-permute-done.11
  293.0 7.2 pad_maximum_fusion
  300.2 30.5 %add_multiply_fusion.14 = f32[64,18,16,128]{3,2,1,0:T(8,128)S(1)} fusion(f32[64,18,16,128]{3,2,1,0:T(8,128)} %pad_maximum_fusion, f32[18]{0:T(128)S(1)} %and_convert_fusion, f32[64,128]{1,0:T(8,128)S(1)} %get-tuple-element.74, f32[64,128]{1,0:T(8,128)S(1)} %get-tuple-element.73, f32[64,16]{1,0:T(8,128)S(1)} %get-tuple-element.72, ...), kind=kLoop, calls=%fused_computation.218 | loop fusion | flops 63700992 | bytes 18957384 | tf_op jit(solution)/shard_map/mul | solution.py:92
  330.8 14.8 %add_multiply_fusion.13 = f32[64,18,16,128]{3,2,1,0:T(8,128)} fusion(f32[64,18,16,128]{3,2,1,0:T(8,128)S(1)} %add_multiply_fusion.14, f32[18]{0:T(128)S(1)} %and_convert_fusion, f32[64,128]{1,0:T(8,128)S(1)} %get-tuple-element.74, f32[64,128]{1,0:T(8,128)S(1)} %get-tuple-element.73, f32[64,16]{1,0:T(8,128)S(1)} %get-tuple-element.72, ...), kind=kLoop, calls=%fused_computation.214 | loop fusion | flops 63700992 | bytes 18957384 | tf_op jit(solution)/shard_map/mul | solution.py:92
  345.6 30.5 %add_multiply_fusion.12 = f32[64,18,16,128]{3,2,1,0:T(8,128)S(1)} fusion(f32[64,18,16,128]{3,2,1,0:T(8,128)} %add_multiply_fusion.13, f32[18]{0:T(128)S(1)} %and_convert_fusion, f32[64,128]{1,0:T(8,128)S(1)} %get-tuple-element.74, f32[64,128]{1,0:T(8,128)S(1)} %get-tuple-element.73, f32[64,16]{1,0:T(8,128)S(1)} %get-tuple-element.72, ...), kind=kLoop, calls=%fused_computation.210 | loop fusion | flops 63700992 | bytes 18957384 | tf_op jit(solution)/shard_map/mul | solution.py:92
  376.1 14.7 %add_multiply_fusion.11 = f32[64,18,16,128]{3,2,1,0:T(8,128)} fusion(f32[64,18,16,128]{3,2,1,0:T(8,128)S(1)} %add_multiply_fusion.12, f32[18]{0:T(128)S(1)} %and_convert_fusion, f32[64,128]{1,0:T(8,128)S(1)} %get-tuple-element.74, f32[64,128]{1,0:T(8,128)S(1)} %get-tuple-element.73, f32[64,16]{1,0:T(8,128)S(1)} %get-tuple-element.72, ...), kind=kLoop, calls=%fused_computation.206 | loop fusion | flops 63700992 | bytes 18957384 | tf_op jit(solution)/shard_map/mul | solution.py:92
  390.9 32.8 %add_multiply_fusion.10 = f32[64,18,16,128]{3,2,1,0:T(8,128)} fusion(f32[64,18,16,128]{3,2,1,0:T(8,128)} %add_multiply_fusion.11, f32[18]{0:T(128)S(1)} %and_convert_fusion, f32[64,128]{1,0:T(8,128)S(1)} %get-tuple-element.74, f32[64,128]{1,0:T(8,128)S(1)} %get-tuple-element.73, f32[64,16]{1,0:T(8,128)S(1)} %get-tuple-element.72, ...), kind=kLoop, calls=%fused_computation.202 | loop fusion | flops 63700992 | bytes 18957384 | tf_op jit(solution)/shard_map/mul | solution.py:92
  423.7 66.0 %subtract_add_fusion.5 = (f32[64,18,16,128]{3,2,1,0:T(8,128)}, f32[64,18,16,128]{3,2,1,0:T(8,128)}, f32[64,18,16,128]{3,2,1,0:T(8,128)}, f32[64,18,16,128]{3,2,1...) fusion(f32[64,18,16,128]{3,2,1,0:T(8,128)} %add_multiply_fusion.10, ...), kind=kLoop, calls=%fused_computation.201 | loop fusion | flops 40108032 | bytes 75580416 | tf_op jit(solution)/shard_map/add | solution.py:50
  489.7 9.3 fusion.50
  499.0 69.0 %conditional.5 = (f32[64,6,16,128]{3,2,1,0:T(8,128)}) conditional(s32[]{:T(128)} %bitcast.30, f32[64,6,16,128]{3,2,1,0:T(8,128)S(1)} %fusion.50, f32[64,6,16,128]{3,2,1,0:T(8,128)S(1)} %fusion.50, f32[64,6,16,128]{3,2,1,0:T(8,128)S(1)} %fusion.50, f32[64,6,16,128]{3,2,1,0:T(8,128)S(1)} %fusion.50), branch_computations={%region_5.6_spmd, %region_6.7_spmd, %region_7.8_spmd, %region_8.9_... | conditional | bytes 12582960 | solution.py:95
  500.3 67.7 %collective-permute-done.2 = f32[64,6,16,128]{3,2,1,0:T(8,128)} collective-permute-done((f32[64,6,16,128]{3,2,1,0:T(8,128)S(1)}, f32[64,6,16,128]{3,2,1,0:T(8,128)}, u32[]{:S(2)}, u32[]{:S(2)}) %collective-permute-start.2) | collective-permute-done | bytes 3145760 | tf_op jit(solution)/shard_map/cond/branch_0_fun/ppermute | solution.py:20
  568.0 3.1 subtract_select_fusion.2
  578.9 29.2 %collective-permute-done.12 = f32[64,6,16,128]{3,2,1,0:T(8,128)S(1)} collective-permute-done((f32[64,6,16,128]{3,2,1,0:T(8,128)S(1)}, f32[64,6,16,128]{3,2,1,0:T(8,128)S(1)}, u32[]{:S(2)}, u32[]{:S(2)}) %collective-permute-start.12) | collective-permute-done | bytes 3145760 | tf_op jit(solution)/shard_map/ppermute | solution.py:31
  608.1 4.5 collective-permute-done.13
  612.6 7.2 pad_maximum_fusion.1
  619.8 30.7 %add_multiply_fusion.9 = f32[64,18,16,128]{3,2,1,0:T(8,128)S(1)} fusion(f32[64,18,16,128]{3,2,1,0:T(8,128)} %pad_maximum_fusion.1, f32[18]{0:T(128)S(1)} %and_convert_fusion, f32[64,128]{1,0:T(8,128)S(1)} %get-tuple-element.74, f32[64,128]{1,0:T(8,128)S(1)} %get-tuple-element.73, f32[64,16]{1,0:T(8,128)S(1)} %get-tuple-element.72, ...), kind=kLoop, calls=%fused_computation.193 | loop fusion | flops 63700992 | bytes 18957384 | tf_op jit(solution)/shard_map/mul | solution.py:92
  650.5 14.8 %add_multiply_fusion.8 = f32[64,18,16,128]{3,2,1,0:T(8,128)} fusion(f32[64,18,16,128]{3,2,1,0:T(8,128)S(1)} %add_multiply_fusion.9, f32[18]{0:T(128)S(1)} %and_convert_fusion, f32[64,128]{1,0:T(8,128)S(1)} %get-tuple-element.74, f32[64,128]{1,0:T(8,128)S(1)} %get-tuple-element.73, f32[64,16]{1,0:T(8,128)S(1)} %get-tuple-element.72, ...), kind=kLoop, calls=%fused_computation.189 | loop fusion | flops 63700992 | bytes 18957384 | tf_op jit(solution)/shard_map/mul | solution.py:92
  665.4 30.5 %add_multiply_fusion.7 = f32[64,18,16,128]{3,2,1,0:T(8,128)S(1)} fusion(f32[64,18,16,128]{3,2,1,0:T(8,128)} %add_multiply_fusion.8, f32[18]{0:T(128)S(1)} %and_convert_fusion, f32[64,128]{1,0:T(8,128)S(1)} %get-tuple-element.74, f32[64,128]{1,0:T(8,128)S(1)} %get-tuple-element.73, f32[64,16]{1,0:T(8,128)S(1)} %get-tuple-element.72, ...), kind=kLoop, calls=%fused_computation.185 | loop fusion | flops 63700992 | bytes 18957384 | tf_op jit(solution)/shard_map/mul | solution.py:92
  695.9 14.7 %add_multiply_fusion.6 = f32[64,18,16,128]{3,2,1,0:T(8,128)} fusion(f32[64,18,16,128]{3,2,1,0:T(8,128)S(1)} %add_multiply_fusion.7, f32[18]{0:T(128)S(1)} %and_convert_fusion, f32[64,128]{1,0:T(8,128)S(1)} %get-tuple-element.74, f32[64,128]{1,0:T(8,128)S(1)} %get-tuple-element.73, f32[64,16]{1,0:T(8,128)S(1)} %get-tuple-element.72, ...), kind=kLoop, calls=%fused_computation.181 | loop fusion | flops 63700992 | bytes 18957384 | tf_op jit(solution)/shard_map/mul | solution.py:92
  710.7 32.8 %add_multiply_fusion.5 = f32[64,18,16,128]{3,2,1,0:T(8,128)} fusion(f32[64,18,16,128]{3,2,1,0:T(8,128)} %add_multiply_fusion.6, f32[18]{0:T(128)S(1)} %and_convert_fusion, f32[64,128]{1,0:T(8,128)S(1)} %get-tuple-element.74, f32[64,128]{1,0:T(8,128)S(1)} %get-tuple-element.73, f32[64,16]{1,0:T(8,128)S(1)} %get-tuple-element.72, ...), kind=kLoop, calls=%fused_computation.177 | loop fusion | flops 63700992 | bytes 18957384 | tf_op jit(solution)/shard_map/mul | solution.py:92
  743.4 65.8 %subtract_add_fusion.3 = (f32[64,18,16,128]{3,2,1,0:T(8,128)}, f32[64,18,16,128]{3,2,1,0:T(8,128)}, f32[64,18,16,128]{3,2,1,0:T(8,128)}, f32[64,18,16,128]{3,2,1...) fusion(f32[64,18,16,128]{3,2,1,0:T(8,128)} %add_multiply_fusion.5, ...), kind=kLoop, calls=%fused_computation.176 | loop fusion | flops 40108032 | bytes 75580416 | tf_op jit(solution)/shard_map/add | solution.py:50
  809.3 9.3 fusion.45
  830.9 28.7 %collective-permute-done.14 = f32[64,6,16,128]{3,2,1,0:T(8,128)S(1)} collective-permute-done((f32[64,6,16,128]{3,2,1,0:T(8,128)S(1)}, f32[64,6,16,128]{3,2,1,0:T(8,128)S(1)}, u32[]{:S(2)}, u32[]{:S(2)}) %collective-permute-start.14) | collective-permute-done | bytes 3145760 | tf_op jit(solution)/shard_map/ppermute | solution.py:31
  859.7 4.5 collective-permute-done.15
  864.2 7.2 pad_maximum_fusion.2
  871.4 30.8 %add_multiply_fusion.4 = f32[64,18,16,128]{3,2,1,0:T(8,128)S(1)} fusion(f32[64,18,16,128]{3,2,1,0:T(8,128)} %pad_maximum_fusion.2, f32[18]{0:T(128)S(1)} %and_convert_fusion, f32[64,128]{1,0:T(8,128)S(1)} %get-tuple-element.74, f32[64,128]{1,0:T(8,128)S(1)} %get-tuple-element.73, f32[64,16]{1,0:T(8,128)S(1)} %get-tuple-element.72, ...), kind=kLoop, calls=%fused_computation.168 | loop fusion | flops 63700992 | bytes 18957384 | tf_op jit(solution)/shard_map/mul | solution.py:92
  902.2 14.8 %add_multiply_fusion.3 = f32[64,18,16,128]{3,2,1,0:T(8,128)} fusion(f32[64,18,16,128]{3,2,1,0:T(8,128)S(1)} %add_multiply_fusion.4, f32[18]{0:T(128)S(1)} %and_convert_fusion, f32[64,128]{1,0:T(8,128)S(1)} %get-tuple-element.74, f32[64,128]{1,0:T(8,128)S(1)} %get-tuple-element.73, f32[64,16]{1,0:T(8,128)S(1)} %get-tuple-element.72, ...), kind=kLoop, calls=%fused_computation.164 | loop fusion | flops 63700992 | bytes 18957384 | tf_op jit(solution)/shard_map/mul | solution.py:92
  917.0 34.0 %add_multiply_fusion.2 = f32[64,18,16,128]{3,2,1,0:T(8,128)} fusion(f32[64,18,16,128]{3,2,1,0:T(8,128)} %add_multiply_fusion.3, f32[18]{0:T(128)S(1)} %and_convert_fusion, f32[64,128]{1,0:T(8,128)S(1)} %get-tuple-element.74, f32[64,128]{1,0:T(8,128)S(1)} %get-tuple-element.73, f32[64,16]{1,0:T(8,128)S(1)} %get-tuple-element.72, ...), kind=kLoop, calls=%fused_computation.160 | loop fusion | flops 63700992 | bytes 18957384 | tf_op jit(solution)/shard_map/mul | solution.py:92
  951.0 28.9 %add_multiply_fusion.1 = f32[64,18,16,128]{3,2,1,0:T(8,128)S(1)} fusion(f32[64,18,16,128]{3,2,1,0:T(8,128)} %add_multiply_fusion.2, f32[18]{0:T(128)S(1)} %and_convert_fusion, f32[64,128]{1,0:T(8,128)S(1)} %get-tuple-element.74, f32[64,128]{1,0:T(8,128)S(1)} %get-tuple-element.73, f32[64,16]{1,0:T(8,128)S(1)} %get-tuple-element.72, ...), kind=kLoop, calls=%fused_computation.156 | loop fusion | flops 63700992 | bytes 18957384 | tf_op jit(solution)/shard_map/mul | solution.py:92
  979.9 14.8 %add_multiply_fusion = f32[64,18,16,128]{3,2,1,0:T(8,128)} fusion(f32[64,18,16,128]{3,2,1,0:T(8,128)S(1)} %add_multiply_fusion.1, f32[18]{0:T(128)S(1)} %and_convert_fusion, f32[64,128]{1,0:T(8,128)S(1)} %get-tuple-element.74, f32[64,128]{1,0:T(8,128)S(1)} %get-tuple-element.73, f32[64,16]{1,0:T(8,128)S(1)} %get-tuple-element.72, ...), kind=kLoop, calls=%fused_computation.152 | loop fusion | flops 63700992 | bytes 18957384 | tf_op jit(solution)/shard_map/mul | solution.py:92
  994.7 65.9 %subtract_add_fusion.1 = (f32[64,18,16,128]{3,2,1,0:T(8,128)}, f32[64,18,16,128]{3,2,1,0:T(8,128)}, f32[64,18,16,128]{3,2,1,0:T(8,128)}, f32[64,18,16,128]{3,2,1...) fusion(f32[64,18,16,128]{3,2,1,0:T(8,128)} %add_multiply_fusion, ...), kind=kLoop, calls=%fused_computation.151 | loop fusion | flops 40108032 | bytes 75580416 | tf_op jit(solution)/shard_map/add | solution.py:50
  1060.7 9.3 fusion.40
  1069.9 69.0 %conditional.7 = (f32[64,6,16,128]{3,2,1,0:T(8,128)}) conditional(s32[]{:T(128)} %bitcast.20, f32[64,6,16,128]{3,2,1,0:T(8,128)S(1)} %fusion.40, f32[64,6,16,128]{3,2,1,0:T(8,128)S(1)} %fusion.40, f32[64,6,16,128]{3,2,1,0:T(8,128)S(1)} %fusion.40, f32[64,6,16,128]{3,2,1,0:T(8,128)S(1)} %fusion.40), branch_computations={%region_13.14_spmd, %region_14.15_spmd, %region_15.16_spmd, %regio... | conditional | bytes 12582960 | solution.py:95
  1071.2 67.7 %collective-permute-done.7 = f32[64,6,16,128]{3,2,1,0:T(8,128)} collective-permute-done((f32[64,6,16,128]{3,2,1,0:T(8,128)S(1)}, f32[64,6,16,128]{3,2,1,0:T(8,128)}, u32[]{:S(2)}, u32[]{:S(2)}) %collective-permute-start.7) | collective-permute-done | bytes 3145760 | tf_op jit(solution)/shard_map/cond/branch_1_fun/ppermute | solution.py:20
  1139.0 4.8 subtract_select_fusion
  (51 shorter events, 45.2 us)
Async XLA Ops:
  0.0 38.3 %collective-permute-start.8 = (f32[64,6,16,128]{3,2,1,0:T(8,128)}, f32[64,6,16,128]{3,2,1,0:T(8,128)}, u32[]{:S(2)}, u32[]{:S(2)}) collective-permute-start(f32[64,6,16,128]{3,2,1,0:T(8,128)} %param.22), channel_id=1, source_target_pairs={{0,1},{1,2},{2,3},{3,4},{4,5},{5,6},{6,7},{8,9},{9,10},{10,11},{11... | collective-permute-start | bytes 9437192 | tf_op jit(solution)/shard_map/ppermute | solution.py:31
  3.8 38.8 %collective-permute-start.9 = (f32[64,6,16,128]{3,2,1,0:T(8,128)}, f32[64,6,16,128]{3,2,1,0:T(8,128)S(1)}, u32[]{:S(2)}, u32[]{:S(2)}) collective-permute-start(f32[64,6,16,128]{3,2,1,0:T(8,128)} %param.22), channel_id=1, source_target_pairs={{1,0},{2,1},{3,2},{4,3},{5,4},{6,5},{7,6},{9,8},{10,9},{11,10},{12... | collective-permute-start | bytes 9437192 | tf_op jit(solution)/shard_map/ppermute | solution.py:33
  42.8 3.7 copy-start
  250.0 4.3 copy-start.2
  250.0 38.5 %collective-permute-start.10 = (f32[64,6,16,128]{3,2,1,0:T(8,128)S(1)}, f32[64,6,16,128]{3,2,1,0:T(8,128)S(1)}, u32[]{:S(2)}, u32[]{:S(2)}) collective-permute-start(f32[64,6,16,128]{3,2,1,0:T(8,128)S(1)} %subtract_select_fusion.3), channel_id=1, source_target_pairs={{0,1},{1,2},{2,3},{3,4},{4,5},{5,6},{6,7},{8,9},{9,10},{10,11},{11... | collective-permute-start | bytes 9437192 | tf_op jit(solution)/shard_map/ppermute | solution.py:31
  254.3 38.7 %collective-permute-start.11 = (f32[64,6,16,128]{3,2,1,0:T(8,128)S(1)}, f32[64,6,16,128]{3,2,1,0:T(8,128)}, u32[]{:S(2)}, u32[]{:S(2)}) collective-permute-start(f32[64,6,16,128]{3,2,1,0:T(8,128)S(1)} %subtract_select_fusion.3), channel_id=1, source_target_pairs={{1,0},{2,1},{3,2},{4,3},{5,4},{6,5},{7,6},{9,8},{10,9},{11,10},{12... | collective-permute-start | bytes 9437192 | tf_op jit(solution)/shard_map/ppermute | solution.py:33
  499.0 69.0 %collective-permute-start.2 = (f32[64,6,16,128]{3,2,1,0:T(8,128)S(1)}, f32[64,6,16,128]{3,2,1,0:T(8,128)}, u32[]{:S(2)}, u32[]{:S(2)}) collective-permute-start(f32[64,6,16,128]{3,2,1,0:T(8,128)S(1)} %param.4), channel_id=1, source_target_pairs={{0,16},{8,24},{16,0},{24,8},{1,17},{9,25},{17,1},{25,9},{2,18},{10... | collective-permute-start | bytes 9437192 | tf_op jit(solution)/shard_map/cond/branch_0_fun/ppermute | solution.py:20
  571.1 2.8 copy-start.3
  571.1 37.0 %collective-permute-start.12 = (f32[64,6,16,128]{3,2,1,0:T(8,128)S(1)}, f32[64,6,16,128]{3,2,1,0:T(8,128)S(1)}, u32[]{:S(2)}, u32[]{:S(2)}) collective-permute-start(f32[64,6,16,128]{3,2,1,0:T(8,128)S(1)} %subtract_select_fusion.2), channel_id=1, source_target_pairs={{0,1},{1,2},{2,3},{3,4},{4,5},{5,6},{6,7},{8,9},{9,10},{10,11},{11... | collective-permute-start | bytes 9437192 | tf_op jit(solution)/shard_map/ppermute | solution.py:31
  573.9 38.7 %collective-permute-start.13 = (f32[64,6,16,128]{3,2,1,0:T(8,128)S(1)}, f32[64,6,16,128]{3,2,1,0:T(8,128)}, u32[]{:S(2)}, u32[]{:S(2)}) collective-permute-start(f32[64,6,16,128]{3,2,1,0:T(8,128)S(1)} %subtract_select_fusion.2), channel_id=1, source_target_pairs={{1,0},{2,1},{3,2},{4,3},{5,4},{6,5},{7,6},{9,8},{10,9},{11,10},{12... | collective-permute-start | bytes 9437192 | tf_op jit(solution)/shard_map/ppermute | solution.py:33
  823.5 1.9 copy-start.1
  823.5 36.1 %collective-permute-start.14 = (f32[64,6,16,128]{3,2,1,0:T(8,128)S(1)}, f32[64,6,16,128]{3,2,1,0:T(8,128)S(1)}, u32[]{:S(2)}, u32[]{:S(2)}) collective-permute-start(f32[64,6,16,128]{3,2,1,0:T(8,128)S(1)} %subtract_select_fusion.1), channel_id=1, source_target_pairs={{0,1},{1,2},{2,3},{3,4},{4,5},{5,6},{6,7},{8,9},{9,10},{10,11},{11... | collective-permute-start | bytes 9437192 | tf_op jit(solution)/shard_map/ppermute | solution.py:31
  825.5 38.7 %collective-permute-start.15 = (f32[64,6,16,128]{3,2,1,0:T(8,128)S(1)}, f32[64,6,16,128]{3,2,1,0:T(8,128)}, u32[]{:S(2)}, u32[]{:S(2)}) collective-permute-start(f32[64,6,16,128]{3,2,1,0:T(8,128)S(1)} %subtract_select_fusion.1), channel_id=1, source_target_pairs={{1,0},{2,1},{3,2},{4,3},{5,4},{6,5},{7,6},{9,8},{10,9},{11,10},{12... | collective-permute-start | bytes 9437192 | tf_op jit(solution)/shard_map/ppermute | solution.py:33
  1069.9 69.0 %collective-permute-start.7 = (f32[64,6,16,128]{3,2,1,0:T(8,128)S(1)}, f32[64,6,16,128]{3,2,1,0:T(8,128)}, u32[]{:S(2)}, u32[]{:S(2)}) collective-permute-start(f32[64,6,16,128]{3,2,1,0:T(8,128)S(1)} %param.13), channel_id=1, source_target_pairs={{0,8},{8,0},{16,24},{24,16},{1,9},{9,1},{17,25},{25,17},{2,10},{10... | collective-permute-start | bytes 9437192 | tf_op jit(solution)/shard_map/cond/branch_1_fun/ppermute | solution.py:20
where the time goes:
time: 1150 us; the launch traced here: 1140 us
  other arithmetic  841 us (73%)
  waiting for transfers between devices  256 us (22%)
  starting transfers between devices  23.5 us (2%)
  local copies, waits for them, and re-layouts  15.1 us (1%)
    mul x24, other arithmetic, local(): wide = substep(wide, drift_x, drift_y, drift_z) * inside  531 us
    add x4, other arithmetic, along(): upper - 2.0 * field + lower  264 us
    ppermute x2, waiting for transfers between devices, partner(): return lax.ppermute(value, axis, pairs)  135 us
    ppermute x4, waiting for transfers between devices, extended(): lax.ppermute(tail, axis, [(i, (i + 1) % count) for i in range(ends)])  107 us
  transfers between devices with their start and end apart: 10, of which 10 were waited for; matrix products, arithmetic and copies ran while one was open for 2% of the time, Pallas kernels for 0%

commit v1 on v0

v1 whole, which is shorter than its diff:
```python
from functools import partial

import jax
import jax.numpy as jnp
from jax import lax
from jax.experimental import pallas as pl
from jax.experimental.pallas import tpu as pltpu
from jax.sharding import PartitionSpec as P

STATE_BITS = 8
BLOCKS = 4
SUBSTEPS = 6
DIFF = 1.0
TIME_STEP = 0.15
TOP = 2**BLOCKS
GROUP = 4
CHUNK = 8
MESH = pl.DeviceIdType.MESH


class Plan:
    def __init__(self, genes, prots, count, width, size_y, size_z):
        self.genes, self.prots = genes, prots
        self.units = count * genes // TOP
        self.mids = count // self.units
        self.split = self.units // genes
        self.slabs = prots // self.split
        self.width, self.size_y, self.size_z = width, size_y, size_z
        self.cells = width * self.split
        self.total_x = width * prots
        self.halo = SUBSTEPS
        self.first = self.halo + 2
        self.layers = self.cells + 2 * self.first
        assert self.split * genes == self.units and self.slabs * self.split == prots
        assert self.cells >= self.halo
        gene_bits = genes.bit_length() - 1
        self.masks = [
            1 << (gene_bits - 1 - k) if k < gene_bits else 1 << (BLOCKS - 1 - (k - gene_bits))
            for k in range(BLOCKS)
        ]


def body(
    pn, x_ref, rate_ref, levels_ref, on_ref, off_ref, order_ref, out_ref,
    buf, land, tab_u, tab_d, tab_y, tab_z, tab_s,
    in_send, in_recv, out_send, out_recv, halo_send, halo_recv,
):
    g, p = lax.axis_index("gene"), lax.axis_index("prot")
    ny = pn.size_y
    q, r = p // pn.slabs, p % pn.slabs
    unit = g * pn.split + q
    part, sub = p // pn.split, p % pn.split
    home = jnp.logical_and(part == r, True)
    has_left, has_right = r > 0, r < pn.slabs - 1

    def rows(layer, n):
        return pl.ds(pl.multiple_of(layer * ny, ny), n * ny)

    def unit_of(k):
        return lax.rem(unit + k, pn.units)

    def in_target(u):
        return (u // pn.split, (u % pn.split) * pn.slabs + part)

    def source_of(k):
        return lax.rem(g * pn.split + sub + k, pn.units)

    def out_target(u):
        return (u // pn.split, r * pn.split + u % pn.split)

    barrier = pltpu.get_barrier_semaphore()

    def greet(k, carry):
        pl.semaphore_signal(barrier, inc=1, device_id=in_target(unit_of(k)), device_id_type=MESH)
        return carry

    def greet_back(k, carry):
        tgt = out_target(lax.rem(g * pn.split + sub + k, pn.units))
        pl.semaphore_signal(barrier, inc=1, device_id=tgt, device_id_type=MESH)
        return carry

    me_source = g * pn.split + sub
    lax.fori_loop(1, pn.units, greet, 0)
    for k in range(pn.units):
        tgt = out_target(k)

        @pl.when(jnp.logical_or(tgt[0] != g, tgt[1] != p))
        def _(tgt=tgt):
            pl.semaphore_signal(barrier, inc=1, device_id=tgt, device_id_type=MESH)

    @pl.when(jnp.logical_not(home))
    def _():
        pl.semaphore_signal(barrier, inc=1, device_id=in_target(unit), device_id_type=MESH)

    @pl.when(has_left)
    def _():
        pl.semaphore_signal(barrier, inc=1, device_id=(g, p - 1), device_id_type=MESH)

    @pl.when(has_right)
    def _():
        pl.semaphore_signal(barrier, inc=1, device_id=(g, p + 1), device_id_type=MESH)

    expected = (
        2 * pn.units - jnp.where(home, 2, 0)
        + jnp.where(has_left, 1, 0) + jnp.where(has_right, 1, 0)
    )
    pl.semaphore_wait(barrier, expected)

    for mid in range(pn.mids):
        for k in range(1, pn.units):
            u = unit_of(k)
            pltpu.make_async_remote_copy(
                src_ref=x_ref.at[mid, u],
                dst_ref=buf.at[0, mid * pn.genes + g, rows(pn.first + sub * pn.width, pn.width)],
                send_sem=in_send.at[mid, u],
                recv_sem=in_recv.at[mid, me_source],
                device_id=in_target(u),
                device_id_type=MESH,
            ).start()
        own_dst = buf.at[0, mid * pn.genes + g, rows(pn.first + sub * pn.width, pn.width)]

        @pl.when(home)
        def _(mid=mid, own_dst=own_dst):
            pltpu.make_async_copy(x_ref.at[mid, unit], own_dst, in_recv.at[mid, me_source]).start()

        @pl.when(jnp.logical_not(home))
        def _(mid=mid, own_dst=own_dst):
            pltpu.make_async_remote_copy(
                src_ref=x_ref.at[mid, unit],
                dst_ref=own_dst,
                send_sem=in_send.at[mid, unit],
                recv_sem=in_recv.at[mid, me_source],
                device_id=in_target(unit),
                device_id_type=MESH,
            ).start()

    nz = pn.size_z
    full = (pn.layers * ny, nz)
    start_x = r * pn.cells
    cell = lax.broadcasted_iota(jnp.int32, full, 0) // ny - pn.first + start_x
    inside = jnp.logical_and(cell >= 0, cell < pn.total_x)
    coord = (cell.astype(jnp.float32) + 0.5) / pn.total_x
    step_x = 1.0 / pn.total_x
    half = 0.5 * TIME_STEP
    yi = lax.broadcasted_iota(jnp.int32, (ny, nz), 0)
    zi = lax.broadcasted_iota(jnp.int32, (8, nz), 1)
    y_at = (yi.astype(jnp.float32) + 0.5) / ny
    z_at = (zi.astype(jnp.float32) + 0.5) / nz

    zero_side = jnp.zeros((pn.first * ny, nz), jnp.float32)

    def tables(t, carry):
        mid, gene = t // pn.genes, t % pn.genes
        at = gene * (pn.mids * pn.units) + mid * pn.units + unit
        lev = [levels_ref[rate_ref[at * 3 + k]] for k in range(3)]
        tab_u[t] = jnp.where(inside, TIME_STEP * DIFF - half * (lev[0] - (coord + step_x)), 0.0)
        tab_d[t] = jnp.where(inside, TIME_STEP * DIFF + half * (lev[0] - (coord - step_x)), 0.0)
        tab_y[t, 0] = jnp.where(yi < ny - 1, TIME_STEP * DIFF - half * (lev[1] - (y_at + 1.0 / ny)), 0.0)
        tab_y[t, 1] = jnp.where(yi > 0, TIME_STEP * DIFF + half * (lev[1] - (y_at - 1.0 / ny)), 0.0)
        tab_z[t, 0] = jnp.where(zi < nz - 1, TIME_STEP * DIFF - half * (lev[2] - (z_at + 1.0 / nz)), 0.0)
        tab_z[t, 1] = jnp.where(zi > 0, TIME_STEP * DIFF + half * (lev[2] - (z_at - 1.0 / nz)), 0.0)
        for side in range(2):
            buf[side, t, rows(0, pn.first)] = zero_side
            buf[side, t, rows(pn.first + pn.cells, pn.first)] = zero_side
        return carry

    lax.fori_loop(0, TOP, tables, 0)

    own = (pn.cells * ny, nz)
    own_cell = lax.broadcasted_iota(jnp.int32, own, 0) // ny + start_x
    own_x = (own_cell.astype(jnp.float32) + 0.5) / pn.total_x
    hill = 0.1 + own_x * own_x / (0.09 + own_x * own_x)
    for b in range(BLOCKS):
        bit = STATE_BITS - 1 - order_ref[b]
        act = on_ref[bit] * hill
        rate = act + off_ref[bit]
        share = act / rate
        decay = jnp.exp(-rate)
        gone = 1.0 - decay
        up = share * gone
        down = (1.0 - share) * gone
        tab_s[b, 0, 0] = 1.0 - up
        tab_s[b, 0, 1] = down
        tab_s[b, 1, 0] = 1.0 - down
        tab_s[b, 1, 1] = up

    def wait_in(mid):
        def one(k, carry):
            gs, js = k // pn.split, k % pn.split
            dst = buf.at[0, mid * pn.genes + gs, rows(pn.first + js * pn.width, pn.width)]
            pltpu.make_async_copy(x_ref.at[0, 0], dst, in_recv.at[mid, k]).wait()
            return carry

        lax.fori_loop(0, pn.units, one, 0)

    groups = TOP // GROUP

    def edge_copies(side, gr):
        states = pl.ds(gr * GROUP, GROUP)
        right = pltpu.make_async_remote_copy(
            src_ref=buf.at[side, states, rows(pn.first + pn.cells - pn.halo, pn.halo)],
            dst_ref=land.at[side, 0, states],
            send_sem=halo_send.at[side, 0, gr],
            recv_sem=halo_recv.at[side, 0, gr],
            device_id=(g, p + 1),
            device_id_type=MESH,
        )
        left = pltpu.make_async_remote_copy(
            src_ref=buf.at[side, states, rows(pn.first, pn.halo)],
            dst_ref=land.at[side, 1, states],
            send_sem=halo_send.at[side, 1, gr],
            recv_sem=halo_recv.at[side, 1, gr],
            device_id=(g, p - 1),
            device_id_type=MESH,
        )
        return left, right

    def send_edges(side, gr):
        left, right = edge_copies(side, gr)
        pl.when(has_left)(left.start)
        pl.when(has_right)(right.start)

    def take_edges(side, gr):
        left, right = edge_copies(side, gr)

        @pl.when(has_left)
        def _():
            right.wait_recv()
            left.wait_send()

        @pl.when(has_right)
        def _():
            left.wait_recv()
            right.wait_send()

        def place(i, carry):
            t = gr * GROUP + i

            @pl.when(has_left)
            def _():
                buf[side, t, rows(pn.first - pn.halo, pn.halo)] = land[side, 0, t]

            @pl.when(has_right)
            def _():
                buf[side, t, rows(pn.first + pn.cells, pn.halo)] = land[side, 1, t]

            return carry

        lax.fori_loop(0, GROUP, place, 0)

    def update(src, dst, t, start, n, cy, cz):
        at = start * ny
        size = n * ny

        def read(off):
            return buf[src, t, pl.ds(at + off, size)]

        here = read(0)
        shape3 = (n, ny, nz)
        out = 0.1 * here if DIFF == 1.0 else (1.0 - 6.0 * TIME_STEP * DIFF) * here
        out = out + tab_u[t, pl.ds(at, size)] * read(ny) + tab_d[t, pl.ds(at, size)] * read(-ny)
        along_y = cy[0][None] * read(1).reshape(shape3) + cy[1][None] * read(-1).reshape(shape3)
        z_next = pltpu.roll(here, nz - 1, 1).reshape(n * ny // 8, 8, nz)
        z_last = pltpu.roll(here, 1, 1).reshape(n * ny // 8, 8, nz)
        along_z = cz[0][None] * z_next + cz[1][None] * z_last
        buf[dst, t, pl.ds(at, size)] = out + along_y.reshape(size, nz) + along_z.reshape(size, nz)

    sides = min(pn.slabs - 1, 2)

    def diffuse(side, t):
        cy = (tab_y[t, 0], tab_y[t, 1])
        cz = (tab_z[t, 0], tab_z[t, 1])
        src, dst = side, 1 - side
        for i in range(SUBSTEPS):
            extra = SUBSTEPS - 1 - i
            if sides == 0:
                begin, n = pn.first, pn.cells
            elif sides == 1:
                begin, n = pn.first - jnp.where(has_left, extra, 0), pn.cells + extra
            else:
                begin, n = pn.first - extra, pn.cells + 2 * extra
            pieces = -(-n // CHUNK)
            done = 0
            for c in range(pieces):
                take = (n - done) // (pieces - c)
                update(src, dst, t, begin + done, take, cy, cz)
                done += take
            src, dst = dst, src

    own_rows = rows(pn.first, pn.cells)

    def switch(b, side, t):
        order = order_ref[b]
        mask = jnp.int32(pn.masks[BLOCKS - 1])
        for k in range(BLOCKS - 1):
            mask = jnp.where(order == k, jnp.int32(pn.masks[k]), mask)
        mate = t ^ mask
        high = jnp.where((t & mask) != 0, 1, 0)
        buf[1 - side, t, own_rows] = (
            tab_s[b, high, 0] * buf[side, t, own_rows] + tab_s[b, high, 1] * buf[side, mate, own_rows]
        )

    waited = 0
    for gr in range(groups):
        need = ((gr + 1) * GROUP - 1) // pn.genes + 1
        while waited < need:
            wait_in(waited)
            waited += 1
        send_edges(0, gr)
        if gr:
            take_edges(0, gr - 1)
            lax.fori_loop(0, GROUP, lambda i, c, gr=gr: (diffuse(0, (gr - 1) * GROUP + i), c)[1], 0)
    take_edges(0, groups - 1)
    lax.fori_loop(0, GROUP, lambda i, c: (diffuse(0, (groups - 1) * GROUP + i), c)[1], 0)

    for b in range(BLOCKS):
        side = b % 2
        after = 1 - side
        last = b == BLOCKS - 1

        def flip(gr, carry, b=b, side=side, after=after, last=last):
            lax.fori_loop(0, GROUP, lambda i, c: (switch(b, side, gr * GROUP + i), c)[1], 0)
            if not last:
                send_edges(after, gr)
            return carry

        def spread(gr, carry, after=after):
            take_edges(after, gr)
            lax.fori_loop(0, GROUP, lambda i, c: (diffuse(after, gr * GROUP + i), c)[1], 0)
            return carry

        if last:
            for gr in range(groups):
                flip(gr, 0)
        else:
            lax.fori_loop(0, groups, flip, 0)
            lax.fori_loop(0, groups, spread, 0)

    fin = BLOCKS % 2

    def out_src(mid, u):
        return buf.at[
            fin, mid * pn.genes + u // pn.split, rows(pn.first + (u % pn.split) * pn.width, pn.width)
        ]

    for mid in range(pn.mids):
        for k in range(pn.units):
            u = lax.rem(unit + k, pn.units)
            tgt = out_target(u)
            mine = jnp.logical_and(tgt[0] == g, tgt[1] == p)

            @pl.when(mine)
            def _(mid=mid, u=u):
                pltpu.make_async_copy(out_src(mid, u), out_ref.at[mid, unit], out_recv.at[mid, unit]).start()

            @pl.when(jnp.logical_not(mine))
            def _(mid=mid, u=u, tgt=tgt):
                pltpu.make_async_remote_copy(
                    src_ref=out_src(mid, u),
                    dst_ref=out_ref.at[mid, unit],
                    send_sem=out_send.at[mid, u],
                    recv_sem=out_recv.at[mid, unit],
                    device_id=tgt,
                    device_id_type=MESH,
                ).start()

    def finish(k, carry):
        tgt = out_target(k)
        for mid in range(pn.mids):
            pltpu.make_async_copy(out_src(mid, 0), out_ref.at[mid, k], out_recv.at[mid, k]).wait()

            @pl.when(jnp.logical_or(tgt[0] != g, tgt[1] != p))
            def _(mid=mid):
                pltpu.make_async_copy(out_src(mid, k), out_ref.at[mid, 0], out_send.at[mid, k]).wait()

            @pl.when(jnp.logical_or(k != unit, jnp.logical_not(home)))
            def _(mid=mid):
                pltpu.make_async_copy(x_ref.at[mid, k], out_src(mid, 0), in_send.at[mid, k]).wait()

        return carry

    lax.fori_loop(0, pn.units, finish, 0)


def local(density, levels, rate_index, on_rate, off_rate, gene_order):
    count, width_x, size_y, size_z = density.shape
    pn = Plan(lax.axis_size("gene"), lax.axis_size("prot"), count, width_x, size_y, size_z)
    rates = lax.all_gather(rate_index.reshape(-1), "gene", tiled=True)
    shape = (pn.mids, pn.units, width_x * size_y, size_z)
    smem = pl.BlockSpec(memory_space=pltpu.SMEM)
    hbm = pl.BlockSpec(memory_space=pl.ANY)
    f32 = jnp.float32
    vec = (pn.layers * size_y, size_z)
    out = pl.pallas_call(
        partial(body, pn),
        out_shape=jax.ShapeDtypeStruct(shape, f32),
        in_specs=[hbm] + [smem] * 5,
        out_specs=hbm,
        scratch_shapes=[
            pltpu.VMEM((2, TOP) + vec, f32),
            pltpu.VMEM((2, 2, TOP, pn.halo * size_y, size_z), f32),
            pltpu.VMEM((TOP,) + vec, f32),
            pltpu.VMEM((TOP,) + vec, f32),
            pltpu.VMEM((TOP, 2, size_y, size_z), f32),
            pltpu.VMEM((TOP, 2, 8, size_z), f32),
            pltpu.VMEM((BLOCKS, 2, 2, pn.cells * size_y, size_z), f32),
            pltpu.SemaphoreType.DMA((pn.mids, pn.units)),
            pltpu.SemaphoreType.DMA((pn.mids, pn.units)),
            pltpu.SemaphoreType.DMA((pn.mids, pn.units)),
            pltpu.SemaphoreType.DMA((pn.mids, pn.units)),
            pltpu.SemaphoreType.DMA((2, 2, TOP // GROUP)),
            pltpu.SemaphoreType.DMA((2, 2, TOP // GROUP)),
        ],
        compiler_params=pltpu.CompilerParams(
            collective_id=0, has_side_effects=True, vmem_limit_bytes=60 * 1024 * 1024
        ),
        name="exchange_evolve",
    )(density.reshape(shape), rates, levels, on_rate, off_rate, gene_order)
    return out.reshape(density.shape)


def solution(mesh):
    in_specs = (P("gene", "prot", None, None), P(), P("gene", None), P(), P(), P())
    out_specs = P("gene", "prot", None, None)
    return jax.shard_map(local, mesh=mesh, in_specs=in_specs, out_specs=out_specs, check_vma=False)
```

time: 1150 us -> 290 us (0.25)
  other arithmetic: 841 us -> 0 us
  Pallas kernels: 0 us -> 276 us
  waiting for transfers between devices: 256 us -> 0 us
  starting transfers between devices: 23.5 us -> 0 us
    mul x24 -> x0, other arithmetic: 531 us -> none  [local(): wide = substep(wide, drift_x, drift_y, drift_z) * inside]
    pallas_call x0 -> x1, Pallas kernels: none -> 276 us  [local(): pl.pallas_call(partial(body, pn), out_shape=jax.ShapeDtypeStruct(shape, f...]
    add x4 -> x0, other arithmetic: 264 us -> none  [along(): upper - 2.0 * field + lower]
    ppermute x10 -> x0, waiting for transfers between devices: 256 us -> none  [the longest x2 135 us: partner(): return lax.ppermute(value, axis, pairs)]
    ppermute x10 -> x0, starting transfers between devices: 23.5 us -> none  [the longest x4 12.8 us: extended(): lax.ppermute(tail, axis, [(i, (i + 1) % count) for i in range(ends)])]
    concatenate x3 -> x0, other arithmetic: 21.6 us -> none  [extended(): jnp.concatenate([lax.ppermute(tail, axis, [(i, (i + 1) % count) for i in...]
    select_n x4 -> x0, other arithmetic: 14.1 us -> none  [local(): field = jnp.where(high, new_high, total - new_high)]
  transfers between devices with their start and end apart: 10 -> 0, of which waited for: 10 -> 0; matrix products, arithmetic and copies ran while one was open for 2% -> 0% of each run, Pallas kernels for 0% -> 0%
where the time goes in v1:
time: 290 us; the launch traced here: 288 us
  Pallas kernels  276 us (95%)
  local copies, waits for them, and re-layouts  6.16 us (2%)
  blocking collectives  5.94 us (2%)
    pallas_call x1, Pallas kernels, local(): pl.pallas_call(partial(body, pn), out_shape=jax.ShapeDtypeStruct(shape, f...  276 us
    unnamed x5, local copies, waits for them, and re-layouts  6.02 us
    unnamed x1, blocking collectives  5.94 us

profile of v1, /device:TPU:9, one launch (start us, length us, event | category | flops | bytes accessed | tf_op | source)
XLA Modules:
  0.0 288.3 jit_solution(3503762439968230836)
XLA Ops:
  0.0 1.2 dynamic-slice
  1.9 0.8 copy.7
  2.7 0.1 reshape.12
  2.8 0.2 dynamic-update-slice
  3.1 5.9 %all-reduce.rate_ref = s32[768]{0:T(1024)} all-reduce(s32[768]{0:T(1024)S(1)} %dynamic-update-slice), channel_id=1, replica_groups=mesh['gene'=4,'prot'=8] {'gene'}, use_global_device_ids=true, to_apply=%add | all-reduce | flops 768 | bytes 6144
  9.0 275.6 %exchange_evolve.1 = f32[4,16,96,128]{3,2,1,0:T(8,128)} custom-call(f32[4,16,96,128]{3,2,1,0:T(8,128)} %bitcast.4, s32[768]{0:T(1024)} %all-reduce.rate_ref, f32[8]{0:T(128)} %levels_ref.1, f32[8]{0:T(128)} %on_ref.1, f32[8]{0:T(128)} %off_ref.1, s32[4]{0:T(128)} %order_ref.1), custom_call_target="tpu_custom_call" | custom-call | tf_op jit(solution)/shard_map/exchange_evolve/pallas_call | solution.py:394
  284.6 3.8 %copy.10 = f32[64,6,16,128]{3,2,1,0:T(8,128)} copy(f32[64,6,16,128]{3,2,1,0:T(8,128)} %bitcast.3) | data formatting | bytes 6291456
  (1 shorter events, 0.0 us)

commit v2 on v1

--- a/solution.py
+++ b/solution.py
@@ -42,7 +42,7 @@
 
 def body(
     pn, x_ref, rate_ref, levels_ref, on_ref, off_ref, order_ref, out_ref,
-    buf, land, tab_u, tab_d, tab_y, tab_z, tab_s,
+    buf, land, tab_u, tab_d, tab_y, tab_z, tab_s, shift, pair,
     in_send, in_recv, out_send, out_recv, halo_send, halo_recv,
 ):
     g, p = lax.axis_index("gene"), lax.axis_index("prot")
@@ -148,6 +148,11 @@
     z_at = (zi.astype(jnp.float32) + 0.5) / nz
 
     zero_side = jnp.zeros((pn.first * ny, nz), jnp.float32)
+
+    from_z = lax.broadcasted_iota(jnp.int32, (2 * nz, 2 * nz), 0) % nz
+    to_z = lax.broadcasted_iota(jnp.int32, (2 * nz, 2 * nz), 1)
+    wanted = jnp.where(to_z < nz, to_z + 1, to_z - nz - 1)
+    shift[...] = jnp.where(from_z == wanted, 1.0, 0.0).astype(shift.dtype)
 
     def tables(t, carry):
         mid, gene = t // pn.genes, t % pn.genes
@@ -248,7 +253,7 @@
 
         lax.fori_loop(0, GROUP, place, 0)
 
-    def update(src, dst, t, start, n, cy, cz):
+    def update(src, dst, t, start, n, cy, cz, z_row):
         at = start * ny
         size = n * ny
 
@@ -260,16 +265,14 @@
         out = 0.1 * here if DIFF == 1.0 else (1.0 - 6.0 * TIME_STEP * DIFF) * here
         out = out + tab_u[t, pl.ds(at, size)] * read(ny) + tab_d[t, pl.ds(at, size)] * read(-ny)
         along_y = cy[0][None] * read(1).reshape(shape3) + cy[1][None] * read(-1).reshape(shape3)
-        z_next = pltpu.roll(here, nz - 1, 1).reshape(n * ny // 8, 8, nz)
-        z_last = pltpu.roll(here, 1, 1).reshape(n * ny // 8, 8, nz)
+        z_next = pair[pl.ds(z_row, size), :nz].reshape(n * ny // 8, 8, nz)
+        z_last = pair[pl.ds(z_row, size), nz:].reshape(n * ny // 8, 8, nz)
         along_z = cz[0][None] * z_next + cz[1][None] * z_last
         buf[dst, t, pl.ds(at, size)] = out + along_y.reshape(size, nz) + along_z.reshape(size, nz)
 
     sides = min(pn.slabs - 1, 2)
 
-    def diffuse(side, t):
-        cy = (tab_y[t, 0], tab_y[t, 1])
-        cz = (tab_z[t, 0], tab_z[t, 1])
+    def diffuse(side, gr):
         src, dst = side, 1 - side
         for i in range(SUBSTEPS):
             extra = SUBSTEPS - 1 - i
@@ -279,12 +282,28 @@
                 begin, n = pn.first - jnp.where(has_left, extra, 0), pn.cells + extra
             else:
                 begin, n = pn.first - extra, pn.cells + 2 * extra
-            pieces = -(-n // CHUNK)
-            done = 0
-            for c in range(pieces):
-                take = (n - done) // (pieces - c)
-                update(src, dst, t, begin + done, take, cy, cz)
-                done += take
+            size = n * ny
+            here = buf[src, pl.ds(gr * GROUP, GROUP), rows(begin, n)].reshape(GROUP * size, nz)
+            high = here.astype(jnp.bfloat16)
+            low = (here - high.astype(jnp.float32)).astype(jnp.bfloat16)
+            pair[pl.ds(0, GROUP * size)] = jnp.dot(
+                jnp.concatenate([high, low], axis=1), shift[...], preferred_element_type=jnp.float32
+            )
+
+            def one(j, carry, src=src, dst=dst, begin=begin, n=n, size=size):
+                t = gr * GROUP + j
+                cy = (tab_y[t, 0], tab_y[t, 1])
+                cz = (tab_z[t, 0], tab_z[t, 1])
+                pieces = -(-n // CHUNK)
+                done = 0
+                for c in range(pieces):
+                    take = (n - done) // (pieces - c)
+                    z_row = pl.multiple_of(j * size + done * ny, ny)
+                    update(src, dst, t, begin + done, take, cy, cz, z_row)
+                    done += take
+                return carry
+
+            lax.fori_loop(0, GROUP, one, 0)
             src, dst = dst, src
 
     own_rows = rows(pn.first, pn.cells)
@@ -300,42 +319,6 @@
             tab_s[b, high, 0] * buf[side, t, own_rows] + tab_s[b, high, 1] * buf[side, mate, own_rows]
         )
 
-    waited = 0
-    for gr in range(groups):
-        need = ((gr + 1) * GROUP - 1) // pn.genes + 1
-        while waited < need:
-            wait_in(waited)
-            waited += 1
-        send_edges(0, gr)
-        if gr:
-            take_edges(0, gr - 1)
-            lax.fori_loop(0, GROUP, lambda i, c, gr=gr: (diffuse(0, (gr - 1) * GROUP + i), c)[1], 0)
-    take_edges(0, groups - 1)
-    lax.fori_loop(0, GROUP, lambda i, c: (diffuse(0, (groups - 1) * GROUP + i), c)[1], 0)
-
-    for b in range(BLOCKS):
-        side = b % 2
-        after = 1 - side
-        last = b == BLOCKS - 1
-
-        def flip(gr, carry, b=b, side=side, after=after, last=last):
-            lax.fori_loop(0, GROUP, lambda i, c: (switch(b, side, gr * GROUP + i), c)[1], 0)
-            if not last:
-                send_edges(after, gr)
-            return carry
-
-        def spread(gr, carry, after=after):
-            take_edges(after, gr)
-            lax.fori_loop(0, GROUP, lambda i, c: (diffuse(after, gr * GROUP + i), c)[1], 0)
-            return carry
-
-        if last:
-            for gr in range(groups):
-                flip(gr, 0)
-        else:
-            lax.fori_loop(0, groups, flip, 0)
-            lax.fori_loop(0, groups, spread, 0)
-
     fin = BLOCKS % 2
 
     def out_src(mid, u):
@@ -343,7 +326,7 @@
             fin, mid * pn.genes + u // pn.split, rows(pn.first + (u % pn.split) * pn.width, pn.width)
         ]
 
-    for mid in range(pn.mids):
+    def send_out(mid):
         for k in range(pn.units):
             u = lax.rem(unit + k, pn.units)
             tgt = out_target(u)
@@ -363,6 +346,58 @@
                     device_id=tgt,
                     device_id_type=MESH,
                 ).start()
+
+    stepwise = pn.genes == GROUP
+    if not stepwise:
+        for mid in range(pn.mids):
+            wait_in(mid)
+
+    def first_block(gr, carry):
+        @pl.when(gr < groups)
+        def _():
+            if stepwise:
+                wait_in(gr)
+            send_edges(0, gr)
+
+        @pl.when(gr > 0)
+        def _():
+            take_edges(0, gr - 1)
+            diffuse(0, gr - 1)
+
+        return carry
+
+    lax.fori_loop(0, groups + 1, first_block, 0)
+
+    def next_block(b, carry):
+        side = lax.rem(b, 2)
+        after = 1 - side
+
+        def flip(gr, c):
+            lax.fori_loop(0, GROUP, lambda i, k: (switch(b, side, gr * GROUP + i), k)[1], 0)
+            send_edges(after, gr)
+            return c
+
+        def spread(gr, c):
+            take_edges(after, gr)
+            diffuse(after, gr)
+            return c
+
+        lax.fori_loop(0, groups, flip, 0)
+        lax.fori_loop(0, groups, spread, 0)
+        return carry
+
+    lax.fori_loop(0, BLOCKS - 1, next_block, 0)
+
+    for gr in range(groups):
+        lax.fori_loop(
+            0, GROUP,
+            lambda i, k, gr=gr: (switch(BLOCKS - 1, (BLOCKS - 1) % 2, gr * GROUP + i), k)[1], 0,
+        )
+        if stepwise:
+            send_out(gr)
+    if not stepwise:
+        for mid in range(pn.mids):
+            send_out(mid)
 
     def finish(k, carry):
         tgt = out_target(k)
@@ -404,6 +439,8 @@
             pltpu.VMEM((TOP, 2, size_y, size_z), f32),
             pltpu.VMEM((TOP, 2, 8, size_z), f32),
             pltpu.VMEM((BLOCKS, 2, 2, pn.cells * size_y, size_z), f32),
+            pltpu.VMEM((2 * size_z, 2 * size_z), jnp.bfloat16),
+            pltpu.VMEM((GROUP * vec[0], 2 * size_z), f32),
             pltpu.SemaphoreType.DMA((pn.mids, pn.units)),
             pltpu.SemaphoreType.DMA((pn.mids, pn.units)),
             pltpu.SemaphoreType.DMA((pn.mids, pn.units)),

time: 290 us -> 256 us (0.88)
  Pallas kernels: 276 us -> 241 us
    pallas_call x1, Pallas kernels: 276 us -> 241 us  [local(): pl.pallas_call(partial(body, pn), out_shape=jax.ShapeDtypeStruct(shape, f...]
where the time goes in v2:
time: 256 us; the launch traced here: 254 us
  Pallas kernels  241 us (94%)
  local copies, waits for them, and re-layouts  6.16 us (2%)
  blocking collectives  5.94 us (2%)
    pallas_call x1, Pallas kernels, local(): pl.pallas_call(partial(body, pn), out_shape=jax.ShapeDtypeStruct(shape, f...  241 us
    unnamed x5, local copies, waits for them, and re-layouts  6.02 us
    unnamed x1, blocking collectives  5.94 us

profile of v2, /device:TPU:9, one launch (start us, length us, event | category | flops | bytes accessed | tf_op | source)
XLA Modules:
  0.0 254.1 jit_solution(8127109045683051638)
XLA Ops:
  0.0 1.2 dynamic-slice
  1.9 0.8 copy.7
  2.7 0.1 reshape.12
  2.8 0.2 dynamic-update-slice
  3.1 5.9 %all-reduce.rate_ref = s32[768]{0:T(1024)} all-reduce(s32[768]{0:T(1024)S(1)} %dynamic-update-slice), channel_id=1, replica_groups=mesh['gene'=4,'prot'=8] {'gene'}, use_global_device_ids=true, to_apply=%add | all-reduce | flops 768 | bytes 6144
  9.0 241.3 %exchange_evolve.1 = f32[4,16,96,128]{3,2,1,0:T(8,128)} custom-call(f32[4,16,96,128]{3,2,1,0:T(8,128)} %bitcast.4, s32[768]{0:T(1024)} %all-reduce.rate_ref, f32[8]{0:T(128)} %levels_ref.1, f32[8]{0:T(128)} %on_ref.1, f32[8]{0:T(128)} %off_ref.1, s32[4]{0:T(128)} %order_ref.1), custom_call_target="tpu_custom_call" | custom-call | tf_op jit(solution)/shard_map/exchange_evolve/pallas_call | solution.py:429
  250.3 3.8 %copy.10 = f32[64,6,16,128]{3,2,1,0:T(8,128)} copy(f32[64,6,16,128]{3,2,1,0:T(8,128)} %bitcast.3) | data formatting | bytes 6291456
  (1 shorter events, 0.0 us)
